TPU v7x, 512 devices: a whole 4x8x8 slice. The times are simulated.
512 devices in a mesh: lat: 32 (over z, x), lon: 16 (over y, core).
Axes of the slice: x: 4, y: 8, z: 8, core: 2. Of those that a mesh axis runs over, the one named last changes fastest.
Arguments:
- state_init: float32 [16, 1048576], P(None, ('lat', 'lon')), may hold values from -6 to 6
- tangent_init: float32 [16, 1048576], P(None, ('lat', 'lon')), may hold values from -6 to 6
- coef_blocks: bfloat16 [8192, 6, 128, 128], P(('lat', 'lon')), may hold values from -0.21875 to 0.21875
- column_lists: int32 [8192, 6], P(('lat', 'lon')), may hold values from 0 to 24, as said below
- send_lists: int32 [512, 4, 2], P(('lat', 'lon')), may hold values from 0 to 15, as said below
- implicit_blocks: bfloat16 [8192, 128, 128], P(('lat', 'lon')), may hold values from -0.5 to 0.5
- uptake_rate: float32 [1048576], P(('lat', 'lon')), may hold values from 0.5 to 4
- coupling: float32 [16, 16], replicated, may hold values from -1.5 to 1.5
- region_map: int32 [1048576], P(('lat', 'lon')), may hold values from 0 to 4095, as said below
- coarse_inverse: float32 [4096, 4096], P(('lat', 'lon')), may hold values from -0.005859375 to 0.005859375
Outputs:
- final_state: float32 [16, 1048576], P(None, ('lat', 'lon'))
- preconditioned: float32 [16, 1048576], P(None, ('lat', 'lon'))
Inputs may be any that keep to these rules, and one draw needn't show every extreme that they name: `column_lists`: entry 0 of row block b's list is b's own index within its tile; entries 1 to 4 lie in the blocks from the lower lat, higher lat, lower lon and higher lon neighbours in that order; the rest are own blocks or 24, the zero block. `send_lists`: indices of the sending tile's own row blocks. `region_map`: region c is owned by tile c // 8; a row's region is owned by its own tile or by one of its two lon neighbours (wrapping).
All inputs are finite; a program needn't handle non-finite values.
Results may differ from a plain program's by a relative error of at most 0.0064.
Values may be sent and summed in bfloat16 or wider, within the bound.
A program may use at most 64 MiB of HBM per device.

v0:
```python
import jax
import jax.numpy as jnp
from jax import lax
from jax.sharding import Mesh
from jax.sharding import PartitionSpec as P

NT = 16
STEPS = 2
REG_DEV = 8
LAT = ("lat_0", "lat_1")
LON = ("lon_0", "lon_1")
LAT_LON = ("lat_0", "lat_1", "lon_0", "lon_1")


step_length = 0.5


def shifted(value, axis, steps):
    count = lax.axis_size(axis)
    first, last = (max(0, -steps), min(count, count - steps))
    return lax.ppermute(value, axis, [(source, source + steps) for source in range(first, last)])


def from_behind(value, axis, steps):
    count = lax.axis_size(axis)
    pairs = [(source, (source + steps) % count) for source in range(count)]
    return lax.ppermute(value, axis, pairs)


def in_order(parts, dim):
    dims = list(parts.shape[1:])
    dims[dim] *= parts.shape[0]
    return jnp.moveaxis(parts, 0, dim).reshape(dims)


def all_blocks(value, axes, sequence):
    parts = value
    for k in sequence:
        parts = lax.all_gather(parts, axes[k])
    done = sequence[::-1]
    back = [done.index(k) for k in range(len(axes))]
    parts = parts.transpose(*back, *range(len(axes), parts.ndim))
    return parts.reshape(-1, *value.shape)


def gather_axes(value, axes, sequence, dim):
    return in_order(all_blocks(value, axes, sequence), dim)


def gather_rims(rounded, sends):
    picked = rounded[:, sends]
    from_below = shifted(picked[:, 0], LAT, 1)
    from_above = shifted(picked[:, 1], LAT, -1)
    from_west = from_behind(picked[:, 2], LON, 1)
    from_east = from_behind(picked[:, 3], LON, -1)
    empty = jnp.zeros((rounded.shape[0], 1, rounded.shape[2]), rounded.dtype)
    return jnp.concatenate([rounded, from_below, from_above, from_west, from_east, empty], axis=1)


def spread_values(own_values, selector):
    lower_values = from_behind(own_values, LON, 1)
    higher_values = from_behind(own_values, LON, -1)
    table = jnp.concatenate([own_values, lower_values, higher_values], axis=1)
    return jnp.dot(
        table, selector, precision=lax.Precision.HIGHEST, preferred_element_type=jnp.float32
    )


def local(
    state_init,
    tangent_init,
    coef_blocks,
    column_lists,
    send_lists,
    implicit_blocks,
    uptake_rate,
    coupling,
    region_map,
    coarse_inverse,
):
    rows = state_init.shape[1]
    blocks = coef_blocks.shape[0]
    block = coef_blocks.shape[2]
    channels = 2 * NT
    sends = send_lists[0]
    state = state_init
    tangent = tangent_init
    for sweep_index in range(STEPS):
        stacked = jnp.concatenate([state, tangent], axis=0)
        rounded = stacked.astype(jnp.bfloat16).reshape(channels, blocks, block)
        readable = gather_rims(rounded, sends)
        gathered = readable[:, column_lists]
        moved = jnp.einsum(
            "cbkp,bkpq->cbq", gathered, coef_blocks, preferred_element_type=jnp.float32
        )
        moved = moved.reshape(channels, rows)
        squared = state * state
        denom = 1.0 + squared
        uptake = uptake_rate * state / denom
        slope = uptake_rate * (1.0 - squared) / (denom * denom) * tangent
        sources = jnp.dot(
            coupling,
            jnp.concatenate([uptake, slope], axis=1),
            precision=lax.Precision.HIGHEST,
            preferred_element_type=jnp.float32,
        )
        sources = jnp.concatenate([sources[:, :rows], sources[:, rows:]], axis=0)
        explicit = (stacked + moved + step_length * sources).astype(jnp.bfloat16)
        implicit = jnp.einsum(
            "cbp,bpq->cbq",
            explicit.reshape(channels, blocks, block),
            implicit_blocks,
            preferred_element_type=jnp.float32,
        )
        implicit = implicit.reshape(channels, rows)
        state = implicit[:NT]
        tangent = implicit[NT:]
    residual = tangent - tangent_init
    lat_pos = lax.axis_index(LAT)
    lon_pos = lax.axis_index(LON)
    lon_count = lax.axis_size(LON)
    tile_self = lat_pos * lon_count + lon_pos
    tile_lower = lat_pos * lon_count + (lon_pos + lon_count - 1) % lon_count
    owner = region_map // REG_DEV
    offset = region_map % REG_DEV
    which = jnp.where(owner == tile_self, 0, jnp.where(owner == tile_lower, 1, 2))
    slot = which * REG_DEV + offset
    selector = (slot[None, :] == jnp.arange(3 * REG_DEV, dtype=jnp.int32)[:, None]).astype(
        jnp.float32
    )
    partial_sums = jnp.dot(
        residual, selector.T, precision=lax.Precision.HIGHEST, preferred_element_type=jnp.float32
    )
    to_lower = partial_sums[:, REG_DEV : 2 * REG_DEV]
    to_higher = partial_sums[:, 2 * REG_DEV :]
    from_higher = from_behind(to_lower, LON, -1)
    from_lower = from_behind(to_higher, LON, 1)
    own_totals = partial_sums[:, :REG_DEV] + from_higher + from_lower
    totals = gather_axes(own_totals, LAT_LON, (1, 0, 2, 3), 1)
    own_values = jnp.dot(
        totals,
        coarse_inverse.T,
        precision=lax.Precision.HIGHEST,
        preferred_element_type=jnp.float32,
    )
    correction = spread_values(own_values, selector)
    preconditioned = residual + correction
    return (state, preconditioned)


def solution(mesh):
    torus = Mesh(mesh.devices.reshape(8, 4, 8, 2), ("lat_0", "lat_1", "lon_0", "lon_1"))
    placed = (
        P(None, LAT_LON),
        P(None, LAT_LON),
        P(LAT_LON, None, None, None),
        P(LAT_LON, None),
        P(LAT_LON, None, None),
        P(LAT_LON, None, None),
        P(LAT_LON),
        P(),
        P(LAT_LON),
        P(LAT_LON, None),
    )
    return jax.shard_map(
        local,
        mesh=torus,
        in_specs=placed,
        out_specs=(P(None, LAT_LON), P(None, LAT_LON)),
        check_vma=False,
    )
```

profile of v0, /device:TPU:1, one launch (start us, length us, event | category | flops | bytes accessed | tf_op | source)
XLA Modules:
  0.0 133.9 jit_solution(14636237051276100255)
XLA Ops:
  0.6 0.8 compare_select_fusion.1
  1.7 0.9 bitcast_dynamic-update-slice_fusion.1
  2.6 0.9 bitcast_dynamic-update-slice_fusion
  3.5 0.7 copy-done.2
  5.4 6.8 %collective-permute-start.3 = (bf16[32,2,128]{2,0,1:T(8,128)(2,1)}, bf16[32,2,128]{2,0,1:T(8,128)(2,1)S(1)}, u32[]{:S(2)}, u32[]{:S(2)}) collective-permute-start(bf16[32,2,128]{2,0,1:T(8,128)(2,1)} %get-tuple-element.22), channel_id=1, source_target_pairs={{0,15},{1,0},{2,1},{3,2},{4,3},{5,4},{6,5},{7,6},{8,7},{9,8},{10,9... | collective-permute-start | bytes 49160 | tf_op jit(solution)/shard_map/ppermute | solution.py:27
  12.3 1.3 collective-permute-start.1
  13.6 4.6 %collective-permute-start = (bf16[32,2,128]{2,0,1:T(8,128)(2,1)}, bf16[32,2,128]{2,0,1:T(8,128)(2,1)}, u32[]{:S(2)}, u32[]{:S(2)}) collective-permute-start(bf16[32,2,128]{2,0,1:T(8,128)(2,1)} %get-tuple-element.25), channel_id=1, source_target_pairs={{0,16},{16,32},{32,48},{48,64},{64,80},{80,96},{96,112},{112,128},... | collective-permute-start | bytes 49160 | tf_op jit(solution)/shard_map/ppermute | solution.py:21
  18.2 0.7 compare_select_fusion
  19.0 1.0 multiply_divide_fusion
  20.1 1.1 convolution_bitcast_fusion.1
  21.8 0.7 fusion.28
  22.6 0.7 constant_dynamic-update-slice_fusion.4
  23.4 1.6 %gather_fusion.1 = bf16[96,32,128]{2,1,0:T(8,128)(2,1)} fusion(bf16[32,25,128]{2,0,1:T(8,128)(2,1)S(1)} %constant_dynamic-update-slice_fusion, s32[1024]{0:T(1024)S(1)} %pad_clamp_fusion), kind=kCustom, calls=%fused_computation.1 | custom fusion | bytes 1573248 | tf_op jit(solution)/shard_map/gather | solution.py:92
  25.0 3.0 %constant_dynamic-update-slice_fusion.11 = (bf16[32,25,128]{2,0,1:T(8,128)(2,1)S(1)}, bf16[32,16,128]{2,0,1:T(8,128)(2,1)}, f32[32,16,128]{2,0,1:T(8,128)}) fusion(bf16[16,128,128]{2,1,0:T(8,128)(2,1)} %param.15, f32[32,16,128]{2,0,1:T(8,128)} %copy-done.2, bf16[32,16,6,128]{3,0,2,1:T(8,128)(2,1)} %bitcast.151, bf16[16,6,128,128]{3,2,1,0:T(8,128)(2,1)S(1)} %copy-done, ...), kind=kOutput, calls=%fused_computation.69 | convolution fusion | flops 117833728 | bytes 5505024 | tf_op jit(solution)/shard_map/cbp,bpq->cbq/dot_general | solution.py:109
  27.9 1.5 %gather_fusion.2 = bf16[8,32,128]{2,1,0:T(8,128)(2,1)S(1)} fusion(bf16[32,16,128]{2,0,1:T(8,128)(2,1)} %get-tuple-element.3, s32[1024]{0:T(1024)S(1)} %pad_clamp_fusion.1), kind=kCustom, calls=%fused_computation.2 | custom fusion | bytes 131104 | tf_op jit(solution)/shard_map/gather | solution.py:51
  29.4 1.1 collective-permute-start.7
  31.2 1.3 collective-permute-start.5
  32.4 4.0 %collective-permute-start.4 = (bf16[32,2,128]{2,0,1:T(8,128)(2,1)S(1)}, bf16[32,2,128]{2,0,1:T(8,128)(2,1)S(1)}, u32[]{:S(2)}, u32[]{:S(2)}) collective-permute-start(bf16[32,2,128]{2,0,1:T(8,128)(2,1)S(1)} %get-tuple-element.21), channel_id=1, source_target_pairs={{0,16},{16,32},{32,48},{48,64},{64,80},{80,96},{96,112},{112,128},... | collective-permute-start | bytes 49160 | tf_op jit(solution)/shard_map/ppermute | solution.py:21
  36.4 1.0 slice_bitcast_fusion.5
  38.7 1.6 %gather_fusion.3 = bf16[96,32,128]{2,1,0:T(8,128)(2,1)} fusion(bf16[32,25,128]{2,0,1:T(8,128)(2,1)S(1)} %constant_dynamic-update-slice_fusion.6, s32[1024]{0:T(1024)S(1)} %pad_clamp_fusion), kind=kCustom, calls=%fused_computation.3 | custom fusion | bytes 1573248 | tf_op jit(solution)/shard_map/gather | solution.py:92
  40.3 2.9 %convolution_bitcast_fusion.2 = f32[32,16,128]{2,0,1:T(8,128)} fusion(bf16[16,128,128]{2,1,0:T(8,128)(2,1)} %param.15, f32[32,16,128]{2,0,1:T(8,128)} %get-tuple-element.28, bf16[32,16,6,128]{3,0,2,1:T(8,128)(2,1)} %bitcast.150, bf16[16,6,128,128]{3,2,1,0:T(8,128)(2,1)S(1)} %copy-done, f32[16,16,128]{2,0,1:T(8,128)} %bitcast.154, ...), kind=kOutput, calls=%fused_computation.7 | convolution fusion | flops 117768192 | bytes 5242880 | tf_op jit(solution)/shard_map/cbp,bpq->cbq/dot_general | solution.py:109
  43.2 1.0 slice_bitcast_fusion
  44.5 1.8 %collective-permute-start.8 = (f32[16,8]{1,0:T(8,128)S(1)}, f32[16,8]{1,0:T(8,128)S(1)}, u32[]{:S(2)}, u32[]{:S(2)}) collective-permute-start(f32[16,8]{1,0:T(8,128)S(1)} %get-tuple-element.26), channel_id=1, source_target_pairs={{0,15},{1,0},{2,1},{3,2},{4,3},{5,4},{6,5},{7,6},{8,7},{9,8},{10,9... | collective-permute-start | bytes 1544 | tf_op jit(solution)/shard_map/ppermute | solution.py:27
  46.3 1.3 collective-permute-done.8
  47.6 1.8 %collective-permute-done.9 = f32[16,8]{1,0:T(8,128)S(1)} collective-permute-done((f32[16,8]{1,0:T(8,128)S(1)}, f32[16,8]{1,0:T(8,128)S(1)}, u32[]{:S(2)}, u32[]{:S(2)}) %collective-permute-start.9) | collective-permute-done | bytes 544 | tf_op jit(solution)/shard_map/ppermute | solution.py:27
  50.0 10.3 %all-gather.4 = f32[4,16,8]{1,2,0:T(8,128)S(1)} all-gather(f32[1,16,8]{1,2,0:T(8,128)} %bitcast.159), channel_id=2, replica_groups=mesh['lat_0'=8,'lat_1'=4,'lon_0'=8,'lon_1'=2] {'lat_1'}, dimensions={0}, use_global_device_ids=true | all-gather | bytes 2560 | tf_op jit(solution)/shard_map/all_gather | solution.py:39
  60.4 26.4 %all-gather.1 = f32[32,16,8]{1,2,0:T(8,128)S(1)} all-gather(f32[4,16,8]{1,2,0:T(8,128)S(1)} %all-gather.4), channel_id=3, replica_groups=mesh['lat_0'=8,'lat_1'=4,'lon_0'=8,'lon_1'=2] {'lat_0'}, dimensions={0}, use_global_device_ids=true | all-gather | bytes 18432 | tf_op jit(solution)/shard_map/all_gather | solution.py:39
  86.7 21.6 %all-gather.2 = f32[64,4,16,8]{2,3,1,0:T(8,128)S(1)} all-gather(f32[8,4,16,8]{2,3,1,0:T(8,128)S(1)} %bitcast.155), channel_id=4, replica_groups=mesh['lat_0'=8,'lat_1'=4,'lon_0'=8,'lon_1'=2] {'lon_0'}, dimensions={0}, use_global_device_ids=true | all-gather | bytes 147456 | tf_op jit(solution)/shard_map/all_gather | solution.py:39
  108.3 20.2 %all-gather.3 = f32[16,8,4,16,8]{3,4,2,1,0:T(8,128)S(1)} all-gather(f32[8,8,4,16,8]{3,4,2,1,0:T(8,128)S(1)} %bitcast.152), channel_id=5, replica_groups=mesh['lat_0'=8,'lat_1'=4,'lon_0'=8,'lon_1'=2] {'lon_1'}, dimensions={0}, use_global_device_ids=true | all-gather | bytes 393216 | tf_op jit(solution)/shard_map/all_gather | solution.py:39
  128.7 1.2 fusion.39
  130.3 1.4 %collective-permute-start.10 = (f32[16,8]{0,1:T(8,128)S(1)}, f32[16,8]{0,1:T(8,128)S(1)}, u32[]{:S(2)}, u32[]{:S(2)}) collective-permute-start(f32[16,8]{0,1:T(8,128)S(1)} %fusion.39), channel_id=1, source_target_pairs={{0,1},{1,2},{2,3},{3,4},{4,5},{5,6},{6,7},{7,8},{8,9},{9,10},{10,1... | collective-permute-start | bytes 1544 | tf_op jit(solution)/shard_map/ppermute | solution.py:27
  133.0 0.9 convolution_add_fusion
  (57 shorter events, 7.1 us)
Async XLA Ops:
  0.6 24.3 %copy-start = (bf16[16,6,128,128]{3,2,1,0:T(8,128)(2,1)S(1)}, bf16[16,6,128,128]{3,2,1,0:T(8,128)(2,1)}, u32[]{:S(2)}) copy-start(bf16[16,6,128,128]{3,2,1,0:T(8,128)(2,1)} %param.12) | copy-start | bytes 9437188
  3.5 0.7 copy-start.2
  5.4 17.9 %collective-permute-start.3 = (bf16[32,2,128]{2,0,1:T(8,128)(2,1)}, bf16[32,2,128]{2,0,1:T(8,128)(2,1)S(1)}, u32[]{:S(2)}, u32[]{:S(2)}) collective-permute-start(bf16[32,2,128]{2,0,1:T(8,128)(2,1)} %get-tuple-element.22), channel_id=1, source_target_pairs={{0,15},{1,0},{2,1},{3,2},{4,3},{5,4},{6,5},{7,6},{8,7},{9,8},{10,9... | collective-permute-start | bytes 49160 | tf_op jit(solution)/shard_map/ppermute | solution.py:27
  12.3 11.0 %collective-permute-start.2 = (bf16[32,2,128]{2,0,1:T(8,128)(2,1)}, bf16[32,2,128]{2,0,1:T(8,128)(2,1)S(1)}, u32[]{:S(2)}, u32[]{:S(2)}) collective-permute-start(bf16[32,2,128]{2,0,1:T(8,128)(2,1)} %get-tuple-element.23), channel_id=1, source_target_pairs={{0,1},{1,2},{2,3},{3,4},{4,5},{5,6},{6,7},{7,8},{8,9},{9,10},{10,1... | collective-permute-start | bytes 49160 | tf_op jit(solution)/shard_map/ppermute | solution.py:27
  12.3 11.0 %collective-permute-start.1 = (bf16[32,2,128]{2,0,1:T(8,128)(2,1)}, bf16[32,2,128]{2,0,1:T(8,128)(2,1)S(1)}, u32[]{:S(2)}, u32[]{:S(2)}) collective-permute-start(bf16[32,2,128]{2,0,1:T(8,128)(2,1)} %get-tuple-element.24), channel_id=1, source_target_pairs={{16,0},{32,16},{48,32},{64,48},{80,64},{96,80},{112,96},{128,112},... | collective-permute-start | bytes 49160 | tf_op jit(solution)/shard_map/ppermute | solution.py:21
  13.6 9.0 %collective-permute-start = (bf16[32,2,128]{2,0,1:T(8,128)(2,1)}, bf16[32,2,128]{2,0,1:T(8,128)(2,1)}, u32[]{:S(2)}, u32[]{:S(2)}) collective-permute-start(bf16[32,2,128]{2,0,1:T(8,128)(2,1)} %get-tuple-element.25), channel_id=1, source_target_pairs={{0,16},{16,32},{32,48},{48,64},{64,80},{80,96},{96,112},{112,128},... | collective-permute-start | bytes 49160 | tf_op jit(solution)/shard_map/ppermute | solution.py:21
  25.0 12.5 %copy-start.4 = (f32[2048]{0:T(1024)S(1)}, f32[2048]{0:T(1024)}, u32[]{:S(2)}) copy-start(f32[2048]{0:T(1024)} %param.16) | copy-start | bytes 24580
  25.0 12.6 %copy-start.5 = (f32[16,16]{1,0:T(8,128)S(1)}, f32[16,16]{1,0:T(8,128)}, u32[]{:S(2)}) copy-start(f32[16,16]{1,0:T(8,128)} %param.17) | copy-start | bytes 3076
  29.4 9.2 %collective-permute-start.7 = (bf16[32,2,128]{2,0,1:T(8,128)(2,1)S(1)}, bf16[32,2,128]{2,0,1:T(8,128)(2,1)S(1)}, u32[]{:S(2)}, u32[]{:S(2)}) collective-permute-start(bf16[32,2,128]{2,0,1:T(8,128)(2,1)S(1)} %get-tuple-element.18), channel_id=1, source_target_pairs={{0,15},{1,0},{2,1},{3,2},{4,3},{5,4},{6,5},{7,6},{8,7},{9,8},{10,9... | collective-permute-start | bytes 49160 | tf_op jit(solution)/shard_map/ppermute | solution.py:27
  30.5 8.1 %collective-permute-start.6 = (bf16[32,2,128]{2,0,1:T(8,128)(2,1)S(1)}, bf16[32,2,128]{2,0,1:T(8,128)(2,1)S(1)}, u32[]{:S(2)}, u32[]{:S(2)}) collective-permute-start(bf16[32,2,128]{2,0,1:T(8,128)(2,1)S(1)} %get-tuple-element.19), channel_id=1, source_target_pairs={{0,1},{1,2},{2,3},{3,4},{4,5},{5,6},{6,7},{7,8},{8,9},{9,10},{10,1... | collective-permute-start | bytes 49160 | tf_op jit(solution)/shard_map/ppermute | solution.py:27
  31.2 7.4 %collective-permute-start.5 = (bf16[32,2,128]{2,0,1:T(8,128)(2,1)S(1)}, bf16[32,2,128]{2,0,1:T(8,128)(2,1)S(1)}, u32[]{:S(2)}, u32[]{:S(2)}) collective-permute-start(bf16[32,2,128]{2,0,1:T(8,128)(2,1)S(1)} %get-tuple-element.20), channel_id=1, source_target_pairs={{16,0},{32,16},{48,32},{64,48},{80,64},{96,80},{112,96},{128,112},... | collective-permute-start | bytes 49160 | tf_op jit(solution)/shard_map/ppermute | solution.py:21
  32.4 6.1 %collective-permute-start.4 = (bf16[32,2,128]{2,0,1:T(8,128)(2,1)S(1)}, bf16[32,2,128]{2,0,1:T(8,128)(2,1)S(1)}, u32[]{:S(2)}, u32[]{:S(2)}) collective-permute-start(bf16[32,2,128]{2,0,1:T(8,128)(2,1)S(1)} %get-tuple-element.21), channel_id=1, source_target_pairs={{0,16},{16,32},{32,48},{48,64},{64,80},{80,96},{96,112},{112,128},... | collective-permute-start | bytes 49160 | tf_op jit(solution)/shard_map/ppermute | solution.py:21
  40.3 3.9 %copy-start.1 = (f32[16,2048]{1,0:T(8,128)S(1)}, f32[16,2048]{1,0:T(8,128)}, u32[]{:S(2)}) copy-start(f32[16,2048]{1,0:T(8,128)} %param.11) | copy-start | bytes 393220
  44.5 3.1 %collective-permute-start.8 = (f32[16,8]{1,0:T(8,128)S(1)}, f32[16,8]{1,0:T(8,128)S(1)}, u32[]{:S(2)}, u32[]{:S(2)}) collective-permute-start(f32[16,8]{1,0:T(8,128)S(1)} %get-tuple-element.26), channel_id=1, source_target_pairs={{0,15},{1,0},{2,1},{3,2},{4,3},{5,4},{6,5},{7,6},{8,7},{9,8},{10,9... | collective-permute-start | bytes 1544 | tf_op jit(solution)/shard_map/ppermute | solution.py:27
  46.3 3.1 %collective-permute-start.9 = (f32[16,8]{1,0:T(8,128)S(1)}, f32[16,8]{1,0:T(8,128)S(1)}, u32[]{:S(2)}, u32[]{:S(2)}) collective-permute-start(f32[16,8]{1,0:T(8,128)S(1)} %get-tuple-element.27), channel_id=1, source_target_pairs={{0,1},{1,2},{2,3},{3,4},{4,5},{5,6},{6,7},{7,8},{8,9},{9,10},{10,1... | collective-permute-start | bytes 1544 | tf_op jit(solution)/shard_map/ppermute | solution.py:27
  108.3 20.5 %copy-start.3 = (f32[8,4096]{1,0:T(8,128)S(1)}, f32[8,4096]{1,0:T(8,128)}, u32[]{:S(2)}) copy-start(f32[8,4096]{1,0:T(8,128)} %param.19) | copy-start | bytes 393220
  129.9 3.1 %collective-permute-start.11 = (f32[16,8]{0,1:T(8,128)S(1)}, f32[16,8]{0,1:T(8,128)S(1)}, u32[]{:S(2)}, u32[]{:S(2)}) collective-permute-start(f32[16,8]{0,1:T(8,128)S(1)} %fusion.39), channel_id=1, source_target_pairs={{0,15},{1,0},{2,1},{3,2},{4,3},{5,4},{6,5},{7,6},{8,7},{9,8},{10,9... | collective-permute-start | bytes 1544 | tf_op jit(solution)/shard_map/ppermute | solution.py:27
  130.3 2.7 %collective-permute-start.10 = (f32[16,8]{0,1:T(8,128)S(1)}, f32[16,8]{0,1:T(8,128)S(1)}, u32[]{:S(2)}, u32[]{:S(2)}) collective-permute-start(f32[16,8]{0,1:T(8,128)S(1)} %fusion.39), channel_id=1, source_target_pairs={{0,1},{1,2},{2,3},{3,4},{4,5},{5,6},{6,7},{7,8},{8,9},{9,10},{10,1... | collective-permute-start | bytes 1544 | tf_op jit(solution)/shard_map/ppermute | solution.py:27
where the time goes:
time: 134 us
  blocking collectives  78.4 us (59%)
  starting transfers between devices  23.3 us (17%)
  local copies, waits for them, and re-layouts  14.6 us (11%)
  matrix products  9.6 us (7%)
  waiting for transfers between devices  3.7 us (3%)
  other arithmetic  3.39 us (3%)
    all_gather x4, blocking collectives, all_blocks(): parts = lax.all_gather(parts, axes[k])  78.4 us
    ppermute x8, starting transfers between devices, from_behind(): return lax.ppermute(value, axis, pairs)  12.2 us
    ppermute x4, starting transfers between devices, shifted(): lax.ppermute(value, axis, [(source, source + steps) for source in range(f...  11.1 us
    dot_general x2, matrix products, local(): jnp.einsum('cbp,bpq->cbq', explicit.reshape(channels, blocks, block), imp...  5.89 us
    unnamed x25, local copies, waits for them, and re-layouts  4.46 us
    ppermute x8, waiting for transfers between devices, from_behind(): return lax.ppermute(value, axis, pairs)  3.69 us
    gather x2, local copies, waits for them, and re-layouts, local(): gathered = readable[:, column_lists]  3.16 us
  transfers between devices with their start and end apart: 12, of which 3 were waited for; matrix products, arithmetic and copies ran while one was open for 6% of the time, Pallas kernels for 0%

commit v1 on v0

v1 whole, which is shorter than its diff:
```python
import jax
import jax.numpy as jnp
from jax import lax
from jax.experimental import pallas as pl
from jax.experimental.pallas import tpu as pltpu
from jax.sharding import Mesh
from jax.sharding import PartitionSpec as P

NT = 16
STEPS = 2
REG_DEV = 8
RB = 16
K = 6
HB = 2
BLOCK = 128
STEP_LENGTH = 0.5
AXES = ("z", "x", "y", "c")
NZ, NX, NY, NCORE = 8, 4, 8, 2
N_LAT = NZ * NX
N_LON = NY * NCORE
MESH = pl.DeviceIdType.MESH
F32 = jnp.float32
BF16 = jnp.bfloat16


def ring_hops(d, n):
    return min(d, n - d)


LON_PEERS = sorted(
    ((dy, dc) for dy in range(NY) for dc in range(NCORE) if (dy, dc) != (0, 0)),
    key=lambda p: -ring_hops(p[0], NY),
)
LAT_PEERS = sorted(
    ((dz, dx) for dz in range(NZ) for dx in range(NX) if (dz, dx) != (0, 0)),
    key=lambda p: -(ring_hops(p[0], NZ) + ring_hops(p[1], NX)),
)


def kernel(
    state_hbm,
    tangent_hbm,
    coef_hbm,
    lists_hbm,
    sends_hbm,
    implicit_hbm,
    rate_hbm,
    coupling_hbm,
    region_hbm,
    coarse_hbm,
    state_out,
    precond_out,
    state0,
    tang0,
    coef,
    impl,
    rate,
    coup,
    region,
    crow_own,
    crow_low,
    crow_high,
    lists,
    sends,
    own_0,
    own_1,
    rims_0,
    rims_1,
    rims_2,
    rims_3,
    rims_4,
    rims_5,
    rims_6,
    rims_7,
    picks,
    acc,
    stk,
    onehot_t,
    onehot,
    coarse_w,
    tile_lon,
    lon_buf,
    tile_lat,
    lat_buf,
    load_sem,
    rim_send,
    rim_recv,
    crow_send,
    crow_recv,
    lon_send,
    lon_recv,
    lat_send,
    lat_recv,
):
    z, x = lax.axis_index("z"), lax.axis_index("x")
    y, c = lax.axis_index("y"), lax.axis_index("c")
    lat = z * NX + x
    lon = y * NCORE + c
    owns = (own_0, own_1)
    rims = ((rims_0, rims_1, rims_2, rims_3), (rims_4, rims_5, rims_6, rims_7))

    def at_lat(v):
        return (v // NX, v % NX, y, c)

    def at_lon(v):
        return (z, x, v // NCORE, v % NCORE)

    def lon_peer(dy, dc):
        return (z, x, (y + dy) % NY, (c + dc) % NCORE)

    def lat_peer(dz, dx):
        return ((z + dz) % NZ, (x + dx) % NX, y, c)

    barrier = pltpu.get_barrier_semaphore()
    for p in LAT_PEERS:
        pl.semaphore_signal(barrier, inc=1, device_id=lat_peer(*p), device_id_type=MESH)
    for p in LON_PEERS:
        pl.semaphore_signal(barrier, inc=1, device_id=lon_peer(*p), device_id_type=MESH)

    pairs = (
        (sends_hbm, sends),
        (state_hbm, state0),
        (tangent_hbm, tang0),
        (lists_hbm, lists),
        (rate_hbm, rate),
        (coupling_hbm, coup),
        (region_hbm, region),
        (coef_hbm, coef),
        (implicit_hbm, impl),
        (coarse_hbm, crow_own),
    )
    loads = [pltpu.make_async_copy(a, b, load_sem.at[i]) for i, (a, b) in enumerate(pairs)]
    for load in loads:
        load.start()

    def cols(b):
        return slice(b * BLOCK, (b + 1) * BLOCK)

    def rim_copies(s):
        below, above = (lat + N_LAT - 1) % N_LAT, (lat + 1) % N_LAT
        west, east = (lon + N_LON - 1) % N_LON, (lon + 1) % N_LON
        targets = (at_lat(above), at_lat(below), at_lon(east), at_lon(west))
        return [
            pltpu.make_async_remote_copy(
                src_ref=picks.at[s, d],
                dst_ref=rims[s][d],
                send_sem=rim_send.at[s, d],
                recv_sem=rim_recv.at[s, d],
                device_id=targets[d],
                device_id_type=MESH,
            )
            for d in range(4)
        ]

    def send_rims(s):
        for d in range(4):
            for h in range(HB):
                picks[s, d, h] = owns[s][sends[0, h, d]]
        copies = rim_copies(s)

        @pl.when(lat < N_LAT - 1)
        def _():
            copies[0].start()

        @pl.when(lat > 0)
        def _():
            copies[1].start()

        copies[2].start()
        copies[3].start()

    def await_rims(s):
        copies = rim_copies(s)

        @pl.when(lat > 0)
        def _():
            copies[0].wait_recv()

        @pl.when(lat < N_LAT - 1)
        def _():
            copies[1].wait_recv()

        copies[2].wait_recv()
        copies[3].wait_recv()

    def await_rim_sends(s):
        copies = rim_copies(s)

        @pl.when(lat < N_LAT - 1)
        def _():
            copies[0].wait_send()

        @pl.when(lat > 0)
        def _():
            copies[1].wait_send()

        copies[2].wait_send()
        copies[3].wait_send()

    zero_block = jnp.zeros((2 * NT, BLOCK), BF16)
    for s in range(STEPS):
        owns[s][RB] = zero_block

    @pl.when(lat == 0)
    def _():
        for s in range(STEPS):
            rims[s][0][...] = jnp.zeros((HB, 2 * NT, BLOCK), BF16)

    @pl.when(lat == N_LAT - 1)
    def _():
        for s in range(STEPS):
            rims[s][1][...] = jnp.zeros((HB, 2 * NT, BLOCK), BF16)

    loads[0].wait()
    loads[1].wait()
    loads[2].wait()
    for b in range(RB):
        own_0[b] = jnp.concatenate([state0[:, cols(b)], tang0[:, cols(b)]], axis=0).astype(BF16)

    pl.semaphore_wait(barrier, len(LAT_PEERS) + len(LON_PEERS))
    send_rims(0)

    loads[9].wait()
    crow_copies = [
        pltpu.make_async_remote_copy(
            src_ref=crow_own,
            dst_ref=dst,
            send_sem=crow_send.at[i],
            recv_sem=crow_recv.at[i],
            device_id=at_lon((lon + step) % N_LON),
            device_id_type=MESH,
        )
        for i, (dst, step) in enumerate(((crow_low, 1), (crow_high, N_LON - 1)))
    ]
    for copy in crow_copies:
        copy.start()

    for i in range(3, 9):
        loads[i].wait()

    lane16 = lax.broadcasted_iota(jnp.int32, (NT, BLOCK), 1)
    row16 = lax.broadcasted_iota(jnp.int32, (NT, BLOCK), 0)
    spread = (lane16 % NT == row16).astype(F32)
    tiled = STEP_LENGTH * jnp.dot(
        coup[...], spread, precision=lax.Precision.HIGHEST, preferred_element_type=F32
    )
    tiled = jnp.concatenate([tiled, tiled], axis=0)
    lane32 = lax.broadcasted_iota(jnp.int32, (2 * NT, BLOCK), 1)
    row32 = lax.broadcasted_iota(jnp.int32, (2 * NT, BLOCK), 0)
    tiled_hi = tiled.astype(BF16).astype(F32)
    tiled_part = jnp.where(lane32 < 64, tiled_hi, tiled - tiled_hi)
    mixer = jnp.where((lane32 % 32) // NT == row32 // NT, tiled_part, 0.0).astype(BF16)

    local_region = region[...] - lat * (N_LON * REG_DEV)
    region_t = jnp.transpose(
        jnp.concatenate([local_region.astype(F32)] * (BLOCK // RB), axis=0), (1, 0)
    )

    def own_part(s):
        for b in range(RB):
            if s == 0:
                st, tg = state0[:, cols(b)], tang0[:, cols(b)]
            else:
                st, tg = stk[b, :NT], stk[b, NT:]
            squared = st * st
            inverse = 1.0 / (1.0 + squared)
            scaled = rate[b : b + 1, :] * inverse
            uptake = scaled * st
            slope = scaled * (1.0 - squared) * inverse * tg
            both = jnp.concatenate([uptake, slope], axis=0)
            both_hi = both.astype(BF16)
            both_lo = (both - both_hi.astype(F32)).astype(BF16)
            sources = jnp.dot(
                mixer,
                jnp.concatenate([both_hi, both_lo, both_hi, both_lo], axis=0),
                preferred_element_type=F32,
            )
            extra = lists[K - 1, b]
            extra = jnp.where(extra >= RB, RB, extra)
            gathered = jnp.concatenate([owns[s][b], owns[s][extra]], axis=1)
            weights = jnp.concatenate([coef[b, 0], coef[b, K - 1]], axis=0)
            moved = jnp.dot(gathered, weights, preferred_element_type=F32)
            acc[b] = jnp.concatenate([st, tg], axis=0) + (moved + sources)

    def rim_part(s, b):
        parts = [rims[s][d][lists[1 + d, b] % HB] for d in range(4)]
        gathered = jnp.concatenate(parts, axis=1)
        weights = coef[b, 1:5].reshape(4 * BLOCK, BLOCK)
        moved = jnp.dot(gathered, weights, preferred_element_type=F32)
        explicit = (acc[b] + moved).astype(BF16)
        return jnp.dot(explicit, impl[b], preferred_element_type=F32)

    own_part(0)
    await_rims(0)
    for b in range(RB):
        new = rim_part(0, b)
        stk[b] = new
        own_1[b] = new.astype(BF16)
    send_rims(1)
    own_part(1)

    lanes = lax.broadcasted_iota(jnp.int32, (BLOCK, BLOCK), 1).astype(F32)
    first = (lat * N_LON + lon - 1) * REG_DEV
    slot = (region[...] - first) & (N_LON * REG_DEV - 1)
    rows = lax.broadcasted_iota(jnp.int32, (32, BLOCK), 0)
    for b in range(RB):
        onehot_t[b] = jnp.where(region_t[:, b : b + 1] == lanes, 1.0, 0.0).astype(BF16)
        onehot[:, cols(b)] = jnp.where(rows == slot[b : b + 1, :], 1.0, 0.0).astype(BF16)

    await_rims(1)
    partial = jnp.zeros((2 * NT, BLOCK), F32)
    for b in range(RB):
        new = rim_part(1, b)
        state_out[:, cols(b)] = new[:NT]
        residual = new[NT:] - tang0[:, cols(b)]
        precond_out[:, cols(b)] = residual
        high = residual.astype(BF16)
        low = (residual - high.astype(F32)).astype(BF16)
        partial += jnp.dot(
            jnp.concatenate([high, low], axis=0), onehot_t[b], preferred_element_type=F32
        )
    partial = partial[:NT] + partial[NT:]
    tile_lon[...] = partial.astype(BF16)

    def peer_copies(src, buf, peers, peer, send_sem, recv_sem):
        return [
            pltpu.make_async_remote_copy(
                src_ref=src,
                dst_ref=buf.at[i],
                send_sem=send_sem.at[i],
                recv_sem=recv_sem.at[i],
                device_id=peer(*p),
                device_id_type=MESH,
            )
            for i, p in enumerate(peers)
        ]

    lon_copies = peer_copies(tile_lon, lon_buf, LON_PEERS, lon_peer, lon_send, lon_recv)
    for copy in lon_copies:
        copy.start()

    for copy in crow_copies:
        copy.wait_recv()
    zero_rows = jnp.zeros((REG_DEV, BLOCK), F32)
    for dz in range(NZ):
        parts = []
        for dx in range(NX):
            other = ((z + NZ - dz) % NZ) * NX + (x + NX - dx) % NX
            at = pl.ds(pl.multiple_of(other * BLOCK, BLOCK), BLOCK)
            parts += [crow_low[:, at], crow_own[:, at], crow_high[:, at], zero_rows]
        coarse_w[dz] = jnp.transpose(jnp.concatenate(parts, axis=0), (1, 0)).astype(BF16)

    totals = partial.astype(BF16).astype(F32)
    for i, copy in enumerate(lon_copies):
        copy.wait_recv()
        totals += lon_buf[i].astype(F32)
    tile_lat[...] = totals.astype(BF16)

    lat_copies = peer_copies(tile_lat, lat_buf, LAT_PEERS, lat_peer, lat_send, lat_recv)
    for copy in lat_copies:
        copy.start()
    for copy in crow_copies + lon_copies:
        copy.wait_send()
    for s in range(STEPS):
        await_rim_sends(s)
    for copy in lat_copies:
        copy.wait_recv()

    values = jnp.zeros((NX * NT, BLOCK), F32)
    for dz in range(NZ):
        tiles = [
            tile_lat[...] if (dz, dx) == (0, 0) else lat_buf[LAT_PEERS.index((dz, dx))]
            for dx in range(NX)
        ]
        values += jnp.dot(
            jnp.concatenate(tiles, axis=0), coarse_w[dz], preferred_element_type=F32
        )
    own_values = values[:NT]
    for dx in range(1, NX):
        own_values += pltpu.roll(values[dx * NT : (dx + 1) * NT], BLOCK - 32 * dx, 1)
    own_values = own_values[:, :32]
    high = own_values.astype(BF16)
    low = (own_values - high.astype(F32)).astype(BF16)
    both = jnp.concatenate([high, low], axis=0)
    for b in range(RB):
        spread_b = jnp.dot(both, onehot[:, cols(b)], preferred_element_type=F32)
        precond_out[:, cols(b)] += spread_b[:NT] + spread_b[NT:]
    for copy in lat_copies:
        copy.wait_send()


def local(
    state_init,
    tangent_init,
    coef_blocks,
    column_lists,
    send_lists,
    implicit_blocks,
    uptake_rate,
    coupling,
    region_map,
    coarse_inverse,
):
    rows = RB * BLOCK
    any_spec = pl.BlockSpec(memory_space=pl.ANY)
    vmem_spec = pl.BlockSpec(memory_space=pltpu.VMEM)
    rim = pltpu.VMEM((HB, 2 * NT, BLOCK), BF16)
    return pl.pallas_call(
        kernel,
        name="tracer_step",
        out_shape=(
            jax.ShapeDtypeStruct((NT, rows), F32),
            jax.ShapeDtypeStruct((NT, rows), F32),
        ),
        in_specs=[any_spec] * 10,
        out_specs=(vmem_spec, vmem_spec),
        scratch_shapes=[
            pltpu.VMEM((NT, rows), F32),
            pltpu.VMEM((NT, rows), F32),
            pltpu.VMEM((RB, K, BLOCK, BLOCK), BF16),
            pltpu.VMEM((RB, BLOCK, BLOCK), BF16),
            pltpu.VMEM((RB, BLOCK), F32),
            pltpu.VMEM((NT, NT), F32),
            pltpu.VMEM((RB, BLOCK), jnp.int32),
            pltpu.VMEM((REG_DEV, N_LAT * BLOCK), F32),
            pltpu.VMEM((REG_DEV, N_LAT * BLOCK), F32),
            pltpu.VMEM((REG_DEV, N_LAT * BLOCK), F32),
            pltpu.SMEM((K, RB), jnp.int32),
            pltpu.SMEM((1, HB, 4), jnp.int32),
            pltpu.VMEM((RB + 1, 2 * NT, BLOCK), BF16),
            pltpu.VMEM((RB + 1, 2 * NT, BLOCK), BF16),
            rim,
            rim,
            rim,
            rim,
            rim,
            rim,
            rim,
            rim,
            pltpu.VMEM((STEPS, 4, HB, 2 * NT, BLOCK), BF16),
            pltpu.VMEM((RB, 2 * NT, BLOCK), F32),
            pltpu.VMEM((RB, 2 * NT, BLOCK), F32),
            pltpu.VMEM((RB, BLOCK, BLOCK), BF16),
            pltpu.VMEM((32, rows), BF16),
            pltpu.VMEM((NZ, BLOCK, BLOCK), BF16),
            pltpu.VMEM((NT, BLOCK), BF16),
            pltpu.VMEM((len(LON_PEERS), NT, BLOCK), BF16),
            pltpu.VMEM((NT, BLOCK), BF16),
            pltpu.VMEM((len(LAT_PEERS), NT, BLOCK), BF16),
            pltpu.SemaphoreType.DMA((10,)),
            pltpu.SemaphoreType.DMA((STEPS, 4)),
            pltpu.SemaphoreType.DMA((STEPS, 4)),
            pltpu.SemaphoreType.DMA((2,)),
            pltpu.SemaphoreType.DMA((2,)),
            pltpu.SemaphoreType.DMA((len(LON_PEERS),)),
            pltpu.SemaphoreType.DMA((len(LON_PEERS),)),
            pltpu.SemaphoreType.DMA((len(LAT_PEERS),)),
            pltpu.SemaphoreType.DMA((len(LAT_PEERS),)),
        ],
        compiler_params=pltpu.CompilerParams(collective_id=0, has_side_effects=True),
    )(
        state_init,
        tangent_init,
        coef_blocks,
        column_lists.T,
        send_lists.transpose(0, 2, 1),
        implicit_blocks,
        uptake_rate.reshape(RB, BLOCK),
        coupling,
        region_map.reshape(RB, BLOCK),
        coarse_inverse,
    )


def solution(mesh):
    torus = Mesh(mesh.devices.reshape(NZ, NX, NY, NCORE), AXES)
    placed = (
        P(None, AXES),
        P(None, AXES),
        P(AXES, None, None, None),
        P(AXES, None),
        P(AXES, None, None),
        P(AXES, None, None),
        P(AXES),
        P(),
        P(AXES),
        P(AXES, None),
    )
    return jax.shard_map(
        local,
        mesh=torus,
        in_specs=placed,
        out_specs=(P(None, AXES), P(None, AXES)),
        check_vma=False,
    )
```

time: 134 us -> 46.2 us (0.34)
  blocking collectives: 78.4 us -> 0 us
  Pallas kernels: 0 us -> 42.2 us
  starting transfers between devices: 23.3 us -> 0 us
  local copies, waits for them, and re-layouts: 14.6 us -> 3.14 us
  matrix products: 9.6 us -> 0 us
  waiting for transfers between devices: 3.7 us -> 0 us
  other arithmetic: 3.39 us -> 0 us
    all_gather x4 -> x0, blocking collectives: 78.4 us -> none  [all_blocks(): parts = lax.all_gather(parts, axes[k])]
    pallas_call x0 -> x1, Pallas kernels: none -> 42.2 us  [local(): pl.pallas_call(kernel, name='tracer_step', out_shape=(jax.ShapeDtypeStruc...]
    ppermute x12 -> x0, starting transfers between devices: 23.3 us -> none  [the longest x8 12.2 us: from_behind(): return lax.ppermute(value, axis, pairs)]
    dot_general x7 -> x0, matrix products: 9.6 us -> none  [the longest x2 5.89 us: local(): jnp.einsum('cbp,bpq->cbq', explicit.reshape(channels, blocks, block), imp...]
    gather x4 -> x0, local copies, waits for them, and re-layouts: 5.19 us -> none  [the longest x2 3.16 us: local(): gathered = readable[:, column_lists]]
    ppermute x12 -> x0, waiting for transfers between devices: 3.7 us -> none  [the longest x8 3.69 us: from_behind(): return lax.ppermute(value, axis, pairs)]
    concatenate x6 -> x0, local copies, waits for them, and re-layouts: 2.29 us -> none  [the longest x3 1.35 us: local(): sources = jnp.concatenate([sources[:, :rows], sources[:, rows:]], axis=0)]
    select_n x2 -> x0, other arithmetic: 1.52 us -> none  [the longest x1 0.83 us: gather_rims(): picked = rounded[:, sends]]
  transfers between devices with their start and end apart: 12 -> 0, of which waited for: 3 -> 0; matrix products, arithmetic and copies ran while one was open for 6% -> 0% of each run, Pallas kernels for 0% -> 0%
where the time goes in v1:
time: 46.2 us; the launch traced here: 46 us
  Pallas kernels  42.2 us (91%)
  local copies, waits for them, and re-layouts  3.14 us (7%)
  between operations  0.64 us (1%)
    pallas_call x1, Pallas kernels, local(): pl.pallas_call(kernel, name='tracer_step', out_shape=(jax.ShapeDtypeStruc...  42.2 us
    unnamed x2, local copies, waits for them, and re-layouts  3.14 us

profile of v1, /device:TPU:1, one launch (start us, length us, event | category | flops | bytes accessed | tf_op | source)
XLA Modules:
  0.0 46.0 jit_solution(10442220962343297676)
XLA Ops:
  0.6 42.2 %tracer_step.1 = (f32[16,2048]{1,0:T(8,128)}, f32[16,2048]{1,0:T(8,128)}) custom-call(f32[16,2048]{1,0:T(8,128)} %state_hbm.1, f32[16,2048]{1,0:T(8,128)} %tangent_hbm.1, bf16[16,6,128,128]{3,2,1,0:T(8,128)(2,1)} %coef_hbm.1, s32[6,16]{1,0:T(8,128)} %bitcast.6, s32[1,2,4]{2,1,0:T(2,128)} %bitcast.7, bf16[16,128,128]{2,1,0:T(8,128)(2,1)} %implicit_hbm.1, ...), custom_call_target="tpu_custom_call" | custom-call | tf_op jit(solution)/shard_map/tracer_step/pallas_call | solution.py:408
  42.9 1.6 %copy.14 = f32[16,2048]{1,0:T(8,128)} copy(f32[16,2048]{1,0:T(8,128)} %get-tuple-element.4) | data formatting | bytes 262144
  44.4 1.6 %copy.15 = f32[16,2048]{1,0:T(8,128)} copy(f32[16,2048]{1,0:T(8,128)} %get-tuple-element.5) | data formatting | bytes 262144

commit v2 on v1

--- a/solution.py
+++ b/solution.py
@@ -74,6 +74,8 @@
     rims_7,
     picks,
     acc,
+    explicit,
+    split,
     stk,
     onehot_t,
     onehot,
@@ -91,6 +93,7 @@
     lon_recv,
     lat_send,
     lat_recv,
+    known,
 ):
     z, x = lax.axis_index("z"), lax.axis_index("x")
     y, c = lax.axis_index("y"), lax.axis_index("c")
@@ -110,12 +113,6 @@
 
     def lat_peer(dz, dx):
         return ((z + dz) % NZ, (x + dx) % NX, y, c)
-
-    barrier = pltpu.get_barrier_semaphore()
-    for p in LAT_PEERS:
-        pl.semaphore_signal(barrier, inc=1, device_id=lat_peer(*p), device_id_type=MESH)
-    for p in LON_PEERS:
-        pl.semaphore_signal(barrier, inc=1, device_id=lon_peer(*p), device_id_type=MESH)
 
     pairs = (
         (sends_hbm, sends),
@@ -132,6 +129,40 @@
     loads = [pltpu.make_async_copy(a, b, load_sem.at[i]) for i, (a, b) in enumerate(pairs)]
     for load in loads:
         load.start()
+
+    def signal(sem, peer):
+        pl.semaphore_signal(sem, inc=1, device_id=peer, device_id_type=MESH)
+
+    def lon_at(step):
+        return at_lon((lon + step + N_LON) % N_LON)
+
+    def z_at(step):
+        return lat_peer(step + NZ, 0)
+
+    def x_at(step):
+        return lat_peer(0, step + NX)
+
+    barrier = pltpu.get_barrier_semaphore()
+    for step in (1, -1):
+        signal(barrier, at_lat((lat + step + N_LAT) % N_LAT))
+        signal(barrier, lon_at(step))
+        signal(barrier, z_at(step))
+        signal(barrier, x_at(step))
+
+    def tell(stage):
+        if stage == 0:
+            told = [(0, lon_at(1)), (0, lon_at(-1)), (1, z_at(1)), (1, z_at(-1))]
+            told += [(2, x_at(1)), (2, x_at(-1))]
+        elif stage == 1:
+            told = [(3, lon_at(2)), (3, lon_at(-2)), (4, z_at(2)), (4, z_at(-2))]
+        else:
+            told = [(5, lon_at(4)), (5, lon_at(-4))] + [(6, x_at(i)) for i in range(1, NX)]
+        for i, peer in told:
+            signal(known.at[i], peer)
+
+    def hear(stage):
+        for i, count in (((0, 2), (1, 2), (2, 2)), ((3, 2), (4, 2)), ((5, 2), (6, NX - 1)))[stage]:
+            pl.semaphore_wait(known.at[i], count)
 
     def cols(b):
         return slice(b * BLOCK, (b + 1) * BLOCK)
@@ -217,10 +248,10 @@
     for b in range(RB):
         own_0[b] = jnp.concatenate([state0[:, cols(b)], tang0[:, cols(b)]], axis=0).astype(BF16)
 
-    pl.semaphore_wait(barrier, len(LAT_PEERS) + len(LON_PEERS))
+    pl.semaphore_wait(barrier, 8)
     send_rims(0)
-
-    loads[9].wait()
+    tell(0)
+
     crow_copies = [
         pltpu.make_async_remote_copy(
             src_ref=crow_own,
@@ -232,8 +263,6 @@
         )
         for i, (dst, step) in enumerate(((crow_low, 1), (crow_high, N_LON - 1)))
     ]
-    for copy in crow_copies:
-        copy.start()
 
     for i in range(3, 9):
         loads[i].wait()
@@ -282,22 +311,33 @@
             moved = jnp.dot(gathered, weights, preferred_element_type=F32)
             acc[b] = jnp.concatenate([st, tg], axis=0) + (moved + sources)
 
-    def rim_part(s, b):
-        parts = [rims[s][d][lists[1 + d, b] % HB] for d in range(4)]
-        gathered = jnp.concatenate(parts, axis=1)
-        weights = coef[b, 1:5].reshape(4 * BLOCK, BLOCK)
-        moved = jnp.dot(gathered, weights, preferred_element_type=F32)
-        explicit = (acc[b] + moved).astype(BF16)
-        return jnp.dot(explicit, impl[b], preferred_element_type=F32)
+    def rim_part(s):
+        for b in range(RB):
+            parts = [rims[s][d][lists[1 + d, b] % HB] for d in range(4)]
+            gathered = jnp.concatenate(parts, axis=1)
+            weights = coef[b, 1:5].reshape(4 * BLOCK, BLOCK)
+            moved = jnp.dot(gathered, weights, preferred_element_type=F32)
+            explicit[b] = (acc[b] + moved).astype(BF16)
+
+    def implicit_part(b):
+        return jnp.dot(explicit[b], impl[b], preferred_element_type=F32)
 
     own_part(0)
+    loads[9].wait()
+    for copy in crow_copies:
+        copy.start()
     await_rims(0)
+    hear(0)
+    tell(1)
+    rim_part(0)
     for b in range(RB):
-        new = rim_part(0, b)
+        new = implicit_part(b)
         stk[b] = new
         own_1[b] = new.astype(BF16)
     send_rims(1)
     own_part(1)
+    hear(1)
+    tell(2)
 
     lanes = lax.broadcasted_iota(jnp.int32, (BLOCK, BLOCK), 1).astype(F32)
     first = (lat * N_LON + lon - 1) * REG_DEV
@@ -308,16 +348,21 @@
         onehot[:, cols(b)] = jnp.where(rows == slot[b : b + 1, :], 1.0, 0.0).astype(BF16)
 
     await_rims(1)
-    partial = jnp.zeros((2 * NT, BLOCK), F32)
+    rim_part(1)
     for b in range(RB):
-        new = rim_part(1, b)
+        new = implicit_part(b)
         state_out[:, cols(b)] = new[:NT]
         residual = new[NT:] - tang0[:, cols(b)]
         precond_out[:, cols(b)] = residual
         high = residual.astype(BF16)
         low = (residual - high.astype(F32)).astype(BF16)
+        split[b] = jnp.concatenate([high, low], axis=0)
+    partial = jnp.zeros((2 * NT, BLOCK), F32)
+    for b in range(0, RB, 2):
         partial += jnp.dot(
-            jnp.concatenate([high, low], axis=0), onehot_t[b], preferred_element_type=F32
+            jnp.concatenate([split[b], split[b + 1]], axis=1),
+            onehot_t[b : b + 2].reshape(2 * BLOCK, BLOCK),
+            preferred_element_type=F32,
         )
     partial = partial[:NT] + partial[NT:]
     tile_lon[...] = partial.astype(BF16)
@@ -335,6 +380,7 @@
             for i, p in enumerate(peers)
         ]
 
+    hear(2)
     lon_copies = peer_copies(tile_lon, lon_buf, LON_PEERS, lon_peer, lon_send, lon_recv)
     for copy in lon_copies:
         copy.start()
@@ -389,6 +435,17 @@
         copy.wait_send()
 
 
+def write_kernel(state_ref, precond_ref, state_out, precond_out, sem):
+    copies = [
+        pltpu.make_async_copy(state_ref, state_out, sem.at[0]),
+        pltpu.make_async_copy(precond_ref, precond_out, sem.at[1]),
+    ]
+    for copy in copies:
+        copy.start()
+    for copy in copies:
+        copy.wait()
+
+
 def local(
     state_init,
     tangent_init,
@@ -402,17 +459,18 @@
     coarse_inverse,
 ):
     rows = RB * BLOCK
-    any_spec = pl.BlockSpec(memory_space=pl.ANY)
+    hbm_spec = pl.BlockSpec(memory_space=pltpu.HBM)
     vmem_spec = pl.BlockSpec(memory_space=pltpu.VMEM)
     rim = pltpu.VMEM((HB, 2 * NT, BLOCK), BF16)
-    return pl.pallas_call(
+    outs = (
+        jax.ShapeDtypeStruct((NT, rows), F32),
+        jax.ShapeDtypeStruct((NT, rows), F32),
+    )
+    results = pl.pallas_call(
         kernel,
         name="tracer_step",
-        out_shape=(
-            jax.ShapeDtypeStruct((NT, rows), F32),
-            jax.ShapeDtypeStruct((NT, rows), F32),
-        ),
-        in_specs=[any_spec] * 10,
+        out_shape=outs,
+        in_specs=[hbm_spec] * 10,
         out_specs=(vmem_spec, vmem_spec),
         scratch_shapes=[
             pltpu.VMEM((NT, rows), F32),
@@ -439,6 +497,8 @@
             rim,
             pltpu.VMEM((STEPS, 4, HB, 2 * NT, BLOCK), BF16),
             pltpu.VMEM((RB, 2 * NT, BLOCK), F32),
+            pltpu.VMEM((RB, 2 * NT, BLOCK), BF16),
+            pltpu.VMEM((RB, 2 * NT, BLOCK), BF16),
             pltpu.VMEM((RB, 2 * NT, BLOCK), F32),
             pltpu.VMEM((RB, BLOCK, BLOCK), BF16),
             pltpu.VMEM((32, rows), BF16),
@@ -456,20 +516,37 @@
             pltpu.SemaphoreType.DMA((len(LON_PEERS),)),
             pltpu.SemaphoreType.DMA((len(LAT_PEERS),)),
             pltpu.SemaphoreType.DMA((len(LAT_PEERS),)),
+            pltpu.SemaphoreType.REGULAR((7,)),
         ],
-        compiler_params=pltpu.CompilerParams(collective_id=0, has_side_effects=True),
+        compiler_params=pltpu.CompilerParams(
+            collective_id=0, has_side_effects=True, vmem_limit_bytes=24 * 2**20
+        ),
     )(
-        state_init,
-        tangent_init,
-        coef_blocks,
-        column_lists.T,
-        send_lists.transpose(0, 2, 1),
-        implicit_blocks,
-        uptake_rate.reshape(RB, BLOCK),
-        coupling,
-        region_map.reshape(RB, BLOCK),
-        coarse_inverse,
-    )
+        *(
+            pltpu.with_memory_space_constraint(value, pltpu.HBM)
+            for value in (
+                state_init,
+                tangent_init,
+                coef_blocks,
+                column_lists.T,
+                send_lists.transpose(0, 2, 1),
+                implicit_blocks,
+                uptake_rate.reshape(RB, BLOCK),
+                coupling,
+                region_map.reshape(RB, BLOCK),
+                coarse_inverse,
+            )
+        )
+    )
+    return pl.pallas_call(
+        write_kernel,
+        name="write_out",
+        out_shape=outs,
+        in_specs=[vmem_spec, vmem_spec],
+        out_specs=(hbm_spec, hbm_spec),
+        scratch_shapes=[pltpu.SemaphoreType.DMA((2,))],
+        compiler_params=pltpu.CompilerParams(vmem_limit_bytes=4 * 2**20),
+    )(*results)
 
 
 def solution(mesh):

time: 46.2 us -> 37.1 us (0.80)
  Pallas kernels: 42.2 us -> 36.4 us
  local copies, waits for them, and re-layouts: 3.14 us -> 0 us
    pallas_call x1 -> x2, Pallas kernels: 42.2 us -> 36.4 us  [the longest x1 35.7 us: local(): pl.pallas_call(kernel, name='tracer_step', out_shape=outs, in_specs=[hbm_...]
    unnamed x2 -> x0, local copies, waits for them, and re-layouts: 3.14 us -> none
where the time goes in v2:
time: 37.1 us; the launch traced here: 37 us
  Pallas kernels  36.4 us (98%)
  between operations  0.64 us (2%)
    pallas_call x1, Pallas kernels, local(): pl.pallas_call(kernel, name='tracer_step', out_shape=outs, in_specs=[hbm_...  35.7 us

profile of v2, /device:TPU:1, one launch (start us, length us, event | category | flops | bytes accessed | tf_op | source)
XLA Modules:
  0.0 37.0 jit_solution(8770754502776940180)
XLA Ops:
  0.6 35.7 %tracer_step.1 = (f32[16,2048]{1,0:T(8,128)S(1)}, f32[16,2048]{1,0:T(8,128)S(1)}) custom-call(f32[16,2048]{1,0:T(8,128)} %state_hbm.1, f32[16,2048]{1,0:T(8,128)} %tangent_hbm.1, bf16[16,6,128,128]{3,2,1,0:T(8,128)(2,1)} %coef_hbm.1, s32[6,16]{1,0:T(8,128)} %bitcast.6, s32[1,2,4]{2,1,0:T(2,128)} %bitcast.7, bf16[16,128,128]{2,1,0:T(8,128)(2,1)} %implicit_hbm.1, ...), custom_call_target="tpu_custom_call" | custom-call | tf_op jit(solution)/shard_map/tracer_step/pallas_call | solution.py:469
  36.3 0.7 %write_out.1 = (f32[16,2048]{1,0:T(8,128)}, f32[16,2048]{1,0:T(8,128)}) custom-call(f32[16,2048]{1,0:T(8,128)S(1)} %get-tuple-element.4.state_ref, f32[16,2048]{1,0:T(8,128)S(1)} %get-tuple-element.5.precond_ref), custom_call_target="tpu_custom_call" | custom-call | tf_op jit(solution)/shard_map/write_out/pallas_call | solution.py:541

commit v3 on v2

--- a/solution.py
+++ b/solution.py
@@ -31,11 +31,6 @@
     ((dy, dc) for dy in range(NY) for dc in range(NCORE) if (dy, dc) != (0, 0)),
     key=lambda p: -ring_hops(p[0], NY),
 )
-LAT_PEERS = sorted(
-    ((dz, dx) for dz in range(NZ) for dx in range(NX) if (dz, dx) != (0, 0)),
-    key=lambda p: -(ring_hops(p[0], NZ) + ring_hops(p[1], NX)),
-)
-
 
 def kernel(
     state_hbm,
@@ -58,8 +53,7 @@
     coup,
     region,
     crow_own,
-    crow_low,
-    crow_high,
+    crow_side,
     lists,
     sends,
     own_0,
@@ -111,7 +105,7 @@
     def lon_peer(dy, dc):
         return (z, x, (y + dy) % NY, (c + dc) % NCORE)
 
-    def lat_peer(dz, dx):
+    def torus_at(dz, dx):
         return ((z + dz) % NZ, (x + dx) % NX, y, c)
 
     pairs = (
@@ -137,10 +131,10 @@
         return at_lon((lon + step + N_LON) % N_LON)
 
     def z_at(step):
-        return lat_peer(step + NZ, 0)
+        return torus_at(step + NZ, 0)
 
     def x_at(step):
-        return lat_peer(0, step + NX)
+        return torus_at(0, step + NX)
 
     barrier = pltpu.get_barrier_semaphore()
     for step in (1, -1):
@@ -151,18 +145,16 @@
 
     def tell(stage):
         if stage == 0:
-            told = [(0, lon_at(1)), (0, lon_at(-1)), (1, z_at(1)), (1, z_at(-1))]
-            told += [(2, x_at(1)), (2, x_at(-1))]
+            told = [lon_at(1), lon_at(-1), z_at(1), z_at(-1), x_at(1), x_at(-1)]
         elif stage == 1:
-            told = [(3, lon_at(2)), (3, lon_at(-2)), (4, z_at(2)), (4, z_at(-2))]
+            told = [lon_at(2), lon_at(-2), z_at(2), z_at(-2)]
         else:
-            told = [(5, lon_at(4)), (5, lon_at(-4))] + [(6, x_at(i)) for i in range(1, NX)]
-        for i, peer in told:
-            signal(known.at[i], peer)
+            told = [lon_at(4), lon_at(-4)] + [x_at(i) for i in range(1, NX)]
+        for peer in told:
+            signal(known.at[stage], peer)
 
     def hear(stage):
-        for i, count in (((0, 2), (1, 2), (2, 2)), ((3, 2), (4, 2)), ((5, 2), (6, NX - 1)))[stage]:
-            pl.semaphore_wait(known.at[i], count)
+        pl.semaphore_wait(known.at[stage], (6, 4, 5)[stage])
 
     def cols(b):
         return slice(b * BLOCK, (b + 1) * BLOCK)
@@ -175,7 +167,7 @@
             pltpu.make_async_remote_copy(
                 src_ref=picks.at[s, d],
                 dst_ref=rims[s][d],
-                send_sem=rim_send.at[s, d],
+                send_sem=rim_send.at[d],
                 recv_sem=rim_recv.at[s, d],
                 device_id=targets[d],
                 device_id_type=MESH,
@@ -255,14 +247,26 @@
     crow_copies = [
         pltpu.make_async_remote_copy(
             src_ref=crow_own,
-            dst_ref=dst,
-            send_sem=crow_send.at[i],
-            recv_sem=crow_recv.at[i],
-            device_id=at_lon((lon + step) % N_LON),
+            dst_ref=crow_side.at[i],
+            send_sem=crow_send,
+            recv_sem=crow_recv,
+            device_id=lon_at(step),
             device_id_type=MESH,
         )
-        for i, (dst, step) in enumerate(((crow_low, 1), (crow_high, N_LON - 1)))
+        for i, step in enumerate((1, -1))
     ]
+
+    def group(ref, send_sem, recv_sem):
+        return pltpu.make_async_remote_copy(
+            src_ref=ref,
+            dst_ref=ref,
+            send_sem=send_sem,
+            recv_sem=recv_sem,
+            device_id=lon_at(1),
+            device_id_type=MESH,
+        )
+
+    crow_all = group(crow_side, crow_send, crow_recv)
 
     for i in range(3, 9):
         loads[i].wait()
@@ -326,23 +330,24 @@
     loads[9].wait()
     for copy in crow_copies:
         copy.start()
-    await_rims(0)
     hear(0)
     tell(1)
+    await_rims(0)
     rim_part(0)
     for b in range(RB):
         new = implicit_part(b)
         stk[b] = new
         own_1[b] = new.astype(BF16)
+    await_rim_sends(0)
     send_rims(1)
-    own_part(1)
     hear(1)
     tell(2)
+    own_part(1)
 
     lanes = lax.broadcasted_iota(jnp.int32, (BLOCK, BLOCK), 1).astype(F32)
     first = (lat * N_LON + lon - 1) * REG_DEV
     slot = (region[...] - first) & (N_LON * REG_DEV - 1)
-    rows = lax.broadcasted_iota(jnp.int32, (32, BLOCK), 0)
+    rows = lax.broadcasted_iota(jnp.int32, (BLOCK, BLOCK), 0) % 32
     for b in range(RB):
         onehot_t[b] = jnp.where(region_t[:, b : b + 1] == lanes, 1.0, 0.0).astype(BF16)
         onehot[:, cols(b)] = jnp.where(rows == slot[b : b + 1, :], 1.0, 0.0).astype(BF16)
@@ -367,72 +372,66 @@
     partial = partial[:NT] + partial[NT:]
     tile_lon[...] = partial.astype(BF16)
 
-    def peer_copies(src, buf, peers, peer, send_sem, recv_sem):
-        return [
-            pltpu.make_async_remote_copy(
-                src_ref=src,
-                dst_ref=buf.at[i],
-                send_sem=send_sem.at[i],
-                recv_sem=recv_sem.at[i],
-                device_id=peer(*p),
-                device_id_type=MESH,
-            )
-            for i, p in enumerate(peers)
-        ]
-
     hear(2)
-    lon_copies = peer_copies(tile_lon, lon_buf, LON_PEERS, lon_peer, lon_send, lon_recv)
-    for copy in lon_copies:
-        copy.start()
-
-    for copy in crow_copies:
-        copy.wait_recv()
+    for i, p in enumerate(LON_PEERS):
+        pltpu.make_async_remote_copy(
+            src_ref=tile_lon,
+            dst_ref=lon_buf.at[i],
+            send_sem=lon_send,
+            recv_sem=lon_recv,
+            device_id=lon_peer(*p),
+            device_id_type=MESH,
+        ).start()
+
+    crow_all.wait_recv()
     zero_rows = jnp.zeros((REG_DEV, BLOCK), F32)
-    for dz in range(NZ):
+    for k in range(NZ):
         parts = []
-        for dx in range(NX):
-            other = ((z + NZ - dz) % NZ) * NX + (x + NX - dx) % NX
-            at = pl.ds(pl.multiple_of(other * BLOCK, BLOCK), BLOCK)
-            parts += [crow_low[:, at], crow_own[:, at], crow_high[:, at], zero_rows]
-        coarse_w[dz] = jnp.transpose(jnp.concatenate(parts, axis=0), (1, 0)).astype(BF16)
+        for i in range(NX):
+            at = cols(k * NX + i)
+            parts += [crow_side[0, :, at], crow_own[:, at], crow_side[1, :, at], zero_rows]
+        coarse_w[k] = jnp.transpose(jnp.concatenate(parts, axis=0), (1, 0)).astype(BF16)
 
     totals = partial.astype(BF16).astype(F32)
-    for i, copy in enumerate(lon_copies):
-        copy.wait_recv()
+    lon_all = group(lon_buf, lon_send, lon_recv)
+    lon_all.wait_recv()
+    for i in range(len(LON_PEERS)):
         totals += lon_buf[i].astype(F32)
     tile_lat[...] = totals.astype(BF16)
-
-    lat_copies = peer_copies(tile_lat, lat_buf, LAT_PEERS, lat_peer, lat_send, lat_recv)
-    for copy in lat_copies:
-        copy.start()
-    for copy in crow_copies + lon_copies:
-        copy.wait_send()
-    for s in range(STEPS):
-        await_rim_sends(s)
-    for copy in lat_copies:
-        copy.wait_recv()
-
-    values = jnp.zeros((NX * NT, BLOCK), F32)
-    for dz in range(NZ):
-        tiles = [
-            tile_lat[...] if (dz, dx) == (0, 0) else lat_buf[LAT_PEERS.index((dz, dx))]
-            for dx in range(NX)
-        ]
-        values += jnp.dot(
-            jnp.concatenate(tiles, axis=0), coarse_w[dz], preferred_element_type=F32
-        )
-    own_values = values[:NT]
-    for dx in range(1, NX):
-        own_values += pltpu.roll(values[dx * NT : (dx + 1) * NT], BLOCK - 32 * dx, 1)
-    own_values = own_values[:, :32]
+    lat_buf[lat] = totals.astype(BF16)
+
+    for i in range(N_LAT - 1):
+        peer = jnp.where(lat <= i, i + 1, i)
+        pltpu.make_async_remote_copy(
+            src_ref=tile_lat,
+            dst_ref=lat_buf.at[lat],
+            send_sem=lat_send,
+            recv_sem=lat_recv,
+            device_id=at_lat(peer),
+            device_id_type=MESH,
+        ).start()
+    crow_all.wait_send()
+    lon_all.wait_send()
+    await_rim_sends(1)
+    lat_all = group(lat_buf.at[pl.ds(0, N_LAT - 1)], lat_send, lat_recv)
+    lat_all.wait_recv()
+
+    tiles = [lat_buf[NX * k : NX * (k + 1)].reshape(NX * NT, BLOCK) for k in range(NZ)]
+    values = jnp.dot(
+        jnp.concatenate(tiles, axis=1),
+        coarse_w[...].reshape(NZ * BLOCK, BLOCK),
+        preferred_element_type=F32,
+    )
+    own_values = jnp.where(lane16 // 32 == 0, values[:NT], 0.0)
+    for i in range(1, NX):
+        own_values += jnp.where(lane16 // 32 == i, values[i * NT : (i + 1) * NT], 0.0)
     high = own_values.astype(BF16)
     low = (own_values - high.astype(F32)).astype(BF16)
-    both = jnp.concatenate([high, low], axis=0)
-    for b in range(RB):
-        spread_b = jnp.dot(both, onehot[:, cols(b)], preferred_element_type=F32)
-        precond_out[:, cols(b)] += spread_b[:NT] + spread_b[NT:]
-    for copy in lat_copies:
-        copy.wait_send()
+    spread_values = jnp.dot(
+        jnp.concatenate([high, low], axis=0), onehot[...], preferred_element_type=F32
+    )
+    precond_out[...] += spread_values[:NT] + spread_values[NT:]
+    lat_all.wait_send()
 
 
 def write_kernel(state_ref, precond_ref, state_out, precond_out, sem):
@@ -481,8 +480,7 @@
             pltpu.VMEM((NT, NT), F32),
             pltpu.VMEM((RB, BLOCK), jnp.int32),
             pltpu.VMEM((REG_DEV, N_LAT * BLOCK), F32),
-            pltpu.VMEM((REG_DEV, N_LAT * BLOCK), F32),
-            pltpu.VMEM((REG_DEV, N_LAT * BLOCK), F32),
+            pltpu.VMEM((2, REG_DEV, N_LAT * BLOCK), F32),
             pltpu.SMEM((K, RB), jnp.int32),
             pltpu.SMEM((1, HB, 4), jnp.int32),
             pltpu.VMEM((RB + 1, 2 * NT, BLOCK), BF16),
@@ -501,22 +499,22 @@
             pltpu.VMEM((RB, 2 * NT, BLOCK), BF16),
             pltpu.VMEM((RB, 2 * NT, BLOCK), F32),
             pltpu.VMEM((RB, BLOCK, BLOCK), BF16),
-            pltpu.VMEM((32, rows), BF16),
+            pltpu.VMEM((BLOCK, rows), BF16),
             pltpu.VMEM((NZ, BLOCK, BLOCK), BF16),
             pltpu.VMEM((NT, BLOCK), BF16),
             pltpu.VMEM((len(LON_PEERS), NT, BLOCK), BF16),
             pltpu.VMEM((NT, BLOCK), BF16),
-            pltpu.VMEM((len(LAT_PEERS), NT, BLOCK), BF16),
+            pltpu.VMEM((N_LAT, NT, BLOCK), BF16),
             pltpu.SemaphoreType.DMA((10,)),
+            pltpu.SemaphoreType.DMA((4,)),
             pltpu.SemaphoreType.DMA((STEPS, 4)),
-            pltpu.SemaphoreType.DMA((STEPS, 4)),
-            pltpu.SemaphoreType.DMA((2,)),
-            pltpu.SemaphoreType.DMA((2,)),
-            pltpu.SemaphoreType.DMA((len(LON_PEERS),)),
-            pltpu.SemaphoreType.DMA((len(LON_PEERS),)),
-            pltpu.SemaphoreType.DMA((len(LAT_PEERS),)),
-            pltpu.SemaphoreType.DMA((len(LAT_PEERS),)),
-            pltpu.SemaphoreType.REGULAR((7,)),
+            pltpu.SemaphoreType.DMA,
+            pltpu.SemaphoreType.DMA,
+            pltpu.SemaphoreType.DMA,
+            pltpu.SemaphoreType.DMA,
+            pltpu.SemaphoreType.DMA,
+            pltpu.SemaphoreType.DMA,
+            pltpu.SemaphoreType.REGULAR((3,)),
         ],
         compiler_params=pltpu.CompilerParams(
             collective_id=0, has_side_effects=True, vmem_limit_bytes=24 * 2**20

time: 37.1 us -> 34.9 us (0.941)
  Pallas kernels: 36.4 us -> 34.1 us
    pallas_call x1, Pallas kernels: 35.7 us -> 33.4 us  [local(): pl.pallas_call(kernel, name='tracer_step', out_shape=outs, in_specs=[hbm_...]
where the time goes in v3:
time: 34.9 us; the launch traced here: 34.7 us
  Pallas kernels  34.1 us (98%)
  between operations  0.64 us (2%)
    pallas_call x1, Pallas kernels, local(): pl.pallas_call(kernel, name='tracer_step', out_shape=outs, in_specs=[hbm_...  33.4 us
    pallas_call x1, Pallas kernels, local(): pl.pallas_call(write_kernel, name='write_out', out_shape=outs, in_specs=[...  0.72 us

profile of v3, /device:TPU:1, one launch (start us, length us, event | category | flops | bytes accessed | tf_op | source)
XLA Modules:
  0.0 34.7 jit_solution(10245051494291628974)
XLA Ops:
  0.6 33.4 %tracer_step.1 = (f32[16,2048]{1,0:T(8,128)S(1)}, f32[16,2048]{1,0:T(8,128)S(1)}) custom-call(f32[16,2048]{1,0:T(8,128)} %state_hbm.1, f32[16,2048]{1,0:T(8,128)} %tangent_hbm.1, bf16[16,6,128,128]{3,2,1,0:T(8,128)(2,1)} %coef_hbm.1, s32[6,16]{1,0:T(8,128)} %bitcast.6, s32[1,2,4]{2,1,0:T(2,128)} %bitcast.7, bf16[16,128,128]{2,1,0:T(8,128)(2,1)} %implicit_hbm.1, ...), custom_call_target="tpu_custom_call" | custom-call | tf_op jit(solution)/shard_map/tracer_step/pallas_call | solution.py:468
  34.0 0.7 %write_out.1 = (f32[16,2048]{1,0:T(8,128)}, f32[16,2048]{1,0:T(8,128)}) custom-call(f32[16,2048]{1,0:T(8,128)S(1)} %get-tuple-element.4.state_ref, f32[16,2048]{1,0:T(8,128)S(1)} %get-tuple-element.5.precond_ref), custom_call_target="tpu_custom_call" | custom-call | tf_op jit(solution)/shard_map/write_out/pallas_call | solution.py:539

commit v4 on v3

--- a/solution.py
+++ b/solution.py
@@ -69,7 +69,8 @@
     picks,
     acc,
     explicit,
-    split,
+    folded,
+    rim_w,
     stk,
     onehot_t,
     onehot,
@@ -352,24 +353,32 @@
         onehot_t[b] = jnp.where(region_t[:, b : b + 1] == lanes, 1.0, 0.0).astype(BF16)
         onehot[:, cols(b)] = jnp.where(rows == slot[b : b + 1, :], 1.0, 0.0).astype(BF16)
 
-    await_rims(1)
-    rim_part(1)
     for b in range(RB):
-        new = implicit_part(b)
-        state_out[:, cols(b)] = new[:NT]
-        residual = new[NT:] - tang0[:, cols(b)]
-        precond_out[:, cols(b)] = residual
-        high = residual.astype(BF16)
-        low = (residual - high.astype(F32)).astype(BF16)
-        split[b] = jnp.concatenate([high, low], axis=0)
-    partial = jnp.zeros((2 * NT, BLOCK), F32)
-    for b in range(0, RB, 2):
+        folded[b] = jnp.dot(impl[b], onehot_t[b], preferred_element_type=F32).astype(BF16)
+    partial = jnp.zeros((NT, BLOCK), F32)
+    for b in range(RB):
         partial += jnp.dot(
-            jnp.concatenate([split[b], split[b + 1]], axis=1),
-            onehot_t[b : b + 2].reshape(2 * BLOCK, BLOCK),
+            jnp.concatenate([acc[b, NT:].astype(BF16), -own_0[b, NT:]], axis=1),
+            jnp.concatenate([folded[b], onehot_t[b]], axis=0),
             preferred_element_type=F32,
         )
-    partial = partial[:NT] + partial[NT:]
+    for d in range(4):
+        both = jnp.zeros((BLOCK, BLOCK), F32)
+        second = jnp.zeros((BLOCK, BLOCK), F32)
+        for b in range(RB):
+            product = jnp.dot(coef[b, 1 + d], folded[b], preferred_element_type=F32)
+            both += product
+            second += product * (lists[1 + d, b] % HB).astype(F32)
+        rim_w[HB * d] = (both - second).astype(BF16)
+        rim_w[HB * d + 1] = second.astype(BF16)
+
+    await_rims(1)
+    tangents = [rims[1][d][h, NT:] for d in range(4) for h in range(HB)]
+    partial += jnp.dot(
+        jnp.concatenate(tangents, axis=1),
+        rim_w[...].reshape(4 * HB * BLOCK, BLOCK),
+        preferred_element_type=F32,
+    )
     tile_lon[...] = partial.astype(BF16)
 
     hear(2)
@@ -382,6 +391,12 @@
             device_id=lon_peer(*p),
             device_id_type=MESH,
         ).start()
+
+    rim_part(1)
+    for b in range(RB):
+        new = implicit_part(b)
+        state_out[:, cols(b)] = new[:NT]
+        precond_out[:, cols(b)] = new[NT:] - tang0[:, cols(b)]
 
     crow_all.wait_recv()
     zero_rows = jnp.zeros((REG_DEV, BLOCK), F32)
@@ -496,7 +511,8 @@
             pltpu.VMEM((STEPS, 4, HB, 2 * NT, BLOCK), BF16),
             pltpu.VMEM((RB, 2 * NT, BLOCK), F32),
             pltpu.VMEM((RB, 2 * NT, BLOCK), BF16),
-            pltpu.VMEM((RB, 2 * NT, BLOCK), BF16),
+            pltpu.VMEM((RB, BLOCK, BLOCK), BF16),
+            pltpu.VMEM((4 * HB, BLOCK, BLOCK), BF16),
             pltpu.VMEM((RB, 2 * NT, BLOCK), F32),
             pltpu.VMEM((RB, BLOCK, BLOCK), BF16),
             pltpu.VMEM((BLOCK, rows), BF16),

time: 34.9 us -> 34 us (0.974)
  Pallas kernels: 34.1 us -> 33.2 us
    pallas_call x1, Pallas kernels: 33.4 us -> 32.5 us  [local(): pl.pallas_call(kernel, name='tracer_step', out_shape=outs, in_specs=[hbm_...]
where the time goes in v4:
time: 34 us; the launch traced here: 33.9 us
  Pallas kernels  33.2 us (98%)
  between operations  0.64 us (2%)
    pallas_call x1, Pallas kernels, local(): pl.pallas_call(kernel, name='tracer_step', out_shape=outs, in_specs=[hbm_...  32.5 us
    pallas_call x1, Pallas kernels, local(): pl.pallas_call(write_kernel, name='write_out', out_shape=outs, in_specs=[...  0.72 us

profile of v4, /device:TPU:1, one launch (start us, length us, event | category | flops | bytes accessed | tf_op | source)
XLA Modules:
  0.0 33.9 jit_solution(2375541582354759945)
XLA Ops:
  0.6 32.5 %tracer_step.1 = (f32[16,2048]{1,0:T(8,128)S(1)}, f32[16,2048]{1,0:T(8,128)S(1)}) custom-call(f32[16,2048]{1,0:T(8,128)} %state_hbm.1, f32[16,2048]{1,0:T(8,128)} %tangent_hbm.1, bf16[16,6,128,128]{3,2,1,0:T(8,128)(2,1)} %coef_hbm.1, s32[6,16]{1,0:T(8,128)} %bitcast.6, s32[1,2,4]{2,1,0:T(2,128)} %bitcast.7, bf16[16,128,128]{2,1,0:T(8,128)(2,1)} %implicit_hbm.1, ...), custom_call_target="tpu_custom_call" | custom-call | tf_op jit(solution)/shard_map/tracer_step/pallas_call | solution.py:483
  33.2 0.7 %write_out.1 = (f32[16,2048]{1,0:T(8,128)}, f32[16,2048]{1,0:T(8,128)}) custom-call(f32[16,2048]{1,0:T(8,128)S(1)} %get-tuple-element.4.state_ref, f32[16,2048]{1,0:T(8,128)S(1)} %get-tuple-element.5.precond_ref), custom_call_target="tpu_custom_call" | custom-call | tf_op jit(solution)/shard_map/write_out/pallas_call | solution.py:555

commit v5 on v4

--- a/solution.py
+++ b/solution.py
@@ -137,25 +137,53 @@
     def x_at(step):
         return torus_at(0, step + NX)
 
+    def signal_z(sem, reach):
+        @pl.when(z + reach < NZ)
+        def _():
+            signal(sem, z_at(reach))
+
+        @pl.when(z >= reach)
+        def _():
+            signal(sem, z_at(-reach))
+
+    def z_count(reach):
+        return jnp.where(z + reach < NZ, 1, 0) + jnp.where(z >= reach, 1, 0)
+
     barrier = pltpu.get_barrier_semaphore()
+
+    @pl.when(lat < N_LAT - 1)
+    def _():
+        signal(barrier, at_lat(lat + 1))
+
+    @pl.when(lat > 0)
+    def _():
+        signal(barrier, at_lat(lat - 1))
+
     for step in (1, -1):
-        signal(barrier, at_lat((lat + step + N_LAT) % N_LAT))
         signal(barrier, lon_at(step))
-        signal(barrier, z_at(step))
         signal(barrier, x_at(step))
+    signal_z(barrier, 1)
+    lat_count = jnp.where(lat < N_LAT - 1, 1, 0) + jnp.where(lat > 0, 1, 0)
 
     def tell(stage):
+        sem = known.at[stage]
+        if stage < 3:
+            signal(sem, lon_at(2**stage))
+            signal(sem, lon_at(-(2**stage)))
         if stage == 0:
-            told = [lon_at(1), lon_at(-1), z_at(1), z_at(-1), x_at(1), x_at(-1)]
-        elif stage == 1:
-            told = [lon_at(2), lon_at(-2), z_at(2), z_at(-2)]
+            signal(sem, x_at(1))
+            signal(sem, x_at(-1))
+        if stage < 2:
+            signal_z(sem, 2**stage)
+        elif stage == 2:
+            signal(sem, z_at(4))
         else:
-            told = [lon_at(4), lon_at(-4)] + [x_at(i) for i in range(1, NX)]
-        for peer in told:
-            signal(known.at[stage], peer)
+            for i in range(1, NX):
+                signal(sem, x_at(i))
 
     def hear(stage):
-        pl.semaphore_wait(known.at[stage], (6, 4, 5)[stage])
+        counts = (4 + z_count(1), 2 + z_count(2), 3, NX - 1)
+        pl.semaphore_wait(known.at[stage], counts[stage])
 
     def cols(b):
         return slice(b * BLOCK, (b + 1) * BLOCK)
@@ -176,10 +204,7 @@
             for d in range(4)
         ]
 
-    def send_rims(s):
-        for d in range(4):
-            for h in range(HB):
-                picks[s, d, h] = owns[s][sends[0, h, d]]
+    def send_lat_rims(s):
         copies = rim_copies(s)
 
         @pl.when(lat < N_LAT - 1)
@@ -190,6 +215,8 @@
         def _():
             copies[1].start()
 
+    def send_lon_rims(s):
+        copies = rim_copies(s)
         copies[2].start()
         copies[3].start()
 
@@ -241,8 +268,12 @@
     for b in range(RB):
         own_0[b] = jnp.concatenate([state0[:, cols(b)], tang0[:, cols(b)]], axis=0).astype(BF16)
 
-    pl.semaphore_wait(barrier, 8)
-    send_rims(0)
+    for d in range(4):
+        for h in range(HB):
+            picks[0, d, h] = own_0[sends[0, h, d]]
+    pl.semaphore_wait(barrier, 4 + lat_count + z_count(1))
+    send_lat_rims(0)
+    send_lon_rims(0)
     tell(0)
 
     crow_copies = [
@@ -316,13 +347,16 @@
             moved = jnp.dot(gathered, weights, preferred_element_type=F32)
             acc[b] = jnp.concatenate([st, tg], axis=0) + (moved + sources)
 
+    def explicit_of(s, b):
+        parts = [rims[s][d][lists[1 + d, b] % HB] for d in range(4)]
+        gathered = jnp.concatenate(parts, axis=1)
+        weights = coef[b, 1:5].reshape(4 * BLOCK, BLOCK)
+        moved = jnp.dot(gathered, weights, preferred_element_type=F32)
+        return (acc[b] + moved).astype(BF16)
+
     def rim_part(s):
         for b in range(RB):
-            parts = [rims[s][d][lists[1 + d, b] % HB] for d in range(4)]
-            gathered = jnp.concatenate(parts, axis=1)
-            weights = coef[b, 1:5].reshape(4 * BLOCK, BLOCK)
-            moved = jnp.dot(gathered, weights, preferred_element_type=F32)
-            explicit[b] = (acc[b] + moved).astype(BF16)
+            explicit[b] = explicit_of(s, b)
 
     def implicit_part(b):
         return jnp.dot(explicit[b], impl[b], preferred_element_type=F32)
@@ -334,15 +368,22 @@
     hear(0)
     tell(1)
     await_rims(0)
+    await_rim_sends(0)
+    for first, send in ((0, send_lat_rims), (2, send_lon_rims)):
+        order = [(d, h, sends[0, h, d]) for d in (first, first + 1) for h in range(HB)]
+        for d, h, b in order:
+            explicit[d * HB + h] = explicit_of(0, b)
+        for d, h, b in order:
+            made = jnp.dot(explicit[d * HB + h], impl[b], preferred_element_type=F32)
+            picks[1, d, h] = made.astype(BF16)
+        send(1)
+    hear(1)
+    tell(2)
     rim_part(0)
     for b in range(RB):
         new = implicit_part(b)
         stk[b] = new
         own_1[b] = new.astype(BF16)
-    await_rim_sends(0)
-    send_rims(1)
-    hear(1)
-    tell(2)
     own_part(1)
 
     lanes = lax.broadcasted_iota(jnp.int32, (BLOCK, BLOCK), 1).astype(F32)
@@ -382,6 +423,7 @@
     tile_lon[...] = partial.astype(BF16)
 
     hear(2)
+    tell(3)
     for i, p in enumerate(LON_PEERS):
         pltpu.make_async_remote_copy(
             src_ref=tile_lon,
@@ -415,6 +457,7 @@
     tile_lat[...] = totals.astype(BF16)
     lat_buf[lat] = totals.astype(BF16)
 
+    hear(3)
     for i in range(N_LAT - 1):
         peer = jnp.where(lat <= i, i + 1, i)
         pltpu.make_async_remote_copy(
@@ -530,7 +573,7 @@
             pltpu.SemaphoreType.DMA,
             pltpu.SemaphoreType.DMA,
             pltpu.SemaphoreType.DMA,
-            pltpu.SemaphoreType.REGULAR((3,)),
+            pltpu.SemaphoreType.REGULAR((4,)),
         ],
         compiler_params=pltpu.CompilerParams(
             collective_id=0, has_side_effects=True, vmem_limit_bytes=24 * 2**20

time: 34 us -> 33.7 us (level)
  no operation moved by 1% of the time
where the time goes in v5:
time: 33.7 us; the launch traced here: 33.6 us
  Pallas kernels  32.9 us (98%)
  between operations  0.64 us (2%)
    pallas_call x1, Pallas kernels, local(): pl.pallas_call(kernel, name='tracer_step', out_shape=outs, in_specs=[hbm_...  32.2 us
    pallas_call x1, Pallas kernels, local(): pl.pallas_call(write_kernel, name='write_out', out_shape=outs, in_specs=[...  0.72 us

profile of v5, /device:TPU:1, one launch (start us, length us, event | category | flops | bytes accessed | tf_op | source)
XLA Modules:
  0.0 33.6 jit_solution(7980784805039645091)
XLA Ops:
  0.6 32.2 %tracer_step.1 = (f32[16,2048]{1,0:T(8,128)S(1)}, f32[16,2048]{1,0:T(8,128)S(1)}) custom-call(f32[16,2048]{1,0:T(8,128)} %state_hbm.1, f32[16,2048]{1,0:T(8,128)} %tangent_hbm.1, bf16[16,6,128,128]{3,2,1,0:T(8,128)(2,1)} %coef_hbm.1, s32[6,16]{1,0:T(8,128)} %bitcast.6, s32[1,2,4]{2,1,0:T(2,128)} %bitcast.7, bf16[16,128,128]{2,1,0:T(8,128)(2,1)} %implicit_hbm.1, ...), custom_call_target="tpu_custom_call" | custom-call | tf_op jit(solution)/shard_map/tracer_step/pallas_call | solution.py:526
  32.9 0.7 %write_out.1 = (f32[16,2048]{1,0:T(8,128)}, f32[16,2048]{1,0:T(8,128)}) custom-call(f32[16,2048]{1,0:T(8,128)S(1)} %get-tuple-element.4.state_ref, f32[16,2048]{1,0:T(8,128)S(1)} %get-tuple-element.5.precond_ref), custom_call_target="tpu_custom_call" | custom-call | tf_op jit(solution)/shard_map/write_out/pallas_call | solution.py:598

commit v6 on v5

--- a/solution.py
+++ b/solution.py
@@ -122,7 +122,16 @@
         (coarse_hbm, crow_own),
     )
     loads = [pltpu.make_async_copy(a, b, load_sem.at[i]) for i, (a, b) in enumerate(pairs)]
-    for load in loads:
+    loads[0].start()
+    half = RB * BLOCK // 2
+    for i in (1, 2):
+        for row in (0, NT // 2):
+            for col in (0, half):
+                piece = (slice(row, row + NT // 2), slice(col, col + half))
+                pltpu.make_async_copy(
+                    pairs[i][0].at[piece], pairs[i][1].at[piece], load_sem.at[i]
+                ).start()
+    for load in loads[3:]:
         load.start()
 
     def signal(sem, peer):
@@ -423,7 +432,6 @@
     tile_lon[...] = partial.astype(BF16)
 
     hear(2)
-    tell(3)
     for i, p in enumerate(LON_PEERS):
         pltpu.make_async_remote_copy(
             src_ref=tile_lon,
@@ -434,6 +442,7 @@
             device_id_type=MESH,
         ).start()
 
+    tell(3)
     rim_part(1)
     for b in range(RB):
         new = implicit_part(b)

time: 33.7 us -> 33.7 us (level)
  no operation moved by 1% of the time
where the time goes in v6:
time: 33.7 us; the launch traced here: 33.6 us
  Pallas kernels  32.9 us (98%)
  between operations  0.64 us (2%)
    pallas_call x1, Pallas kernels, local(): pl.pallas_call(kernel, name='tracer_step', out_shape=outs, in_specs=[hbm_...  32.2 us
    pallas_call x1, Pallas kernels, local(): pl.pallas_call(write_kernel, name='write_out', out_shape=outs, in_specs=[...  0.72 us

profile of v6, /device:TPU:1, one launch (start us, length us, event | category | flops | bytes accessed | tf_op | source)
XLA Modules:
  0.0 33.6 jit_solution(10182211559067015156)
XLA Ops:
  0.6 32.2 %tracer_step.1 = (f32[16,2048]{1,0:T(8,128)S(1)}, f32[16,2048]{1,0:T(8,128)S(1)}) custom-call(f32[16,2048]{1,0:T(8,128)} %state_hbm.1, f32[16,2048]{1,0:T(8,128)} %tangent_hbm.1, bf16[16,6,128,128]{3,2,1,0:T(8,128)(2,1)} %coef_hbm.1, s32[6,16]{1,0:T(8,128)} %bitcast.6, s32[1,2,4]{2,1,0:T(2,128)} %bitcast.7, bf16[16,128,128]{2,1,0:T(8,128)(2,1)} %implicit_hbm.1, ...), custom_call_target="tpu_custom_call" | custom-call | tf_op jit(solution)/shard_map/tracer_step/pallas_call | solution.py:535
  32.9 0.7 %write_out.1 = (f32[16,2048]{1,0:T(8,128)}, f32[16,2048]{1,0:T(8,128)}) custom-call(f32[16,2048]{1,0:T(8,128)S(1)} %get-tuple-element.4.state_ref, f32[16,2048]{1,0:T(8,128)S(1)} %get-tuple-element.5.precond_ref), custom_call_target="tpu_custom_call" | custom-call | tf_op jit(solution)/shard_map/write_out/pallas_call | solution.py:607
